TPU v7x, 32 devices: a whole 2x2x4 slice. The times are simulated.
32 devices in a mesh: gy: 8 (over z, x), gx: 4 (over y, core).
Axes of the slice: x: 2, y: 2, z: 4, core: 2. Of those that a mesh axis runs over, the one named last changes fastest.
Arguments:
- tall_factor: bfloat16 [8192, 2048], P('gy', 'gx'), may hold values from -6 to 6
- wide_factor: bfloat16 [2048, 4096], P('gy', 'gx'), may hold values from -0.125 to 0.125
- target: float32 [8192, 4096], P('gy', 'gx'), may hold values from -6 to 6
Outputs:
- product_sum: float32 [8192, 4096], P('gy', 'gx')
All inputs are finite; a program needn't handle non-finite values.
Results may differ from a plain program's by a relative error of at most 0.0003.
Values may be sent and summed in bfloat16 or wider, within the bound.
A program may use at most 128 MiB of HBM per device.

v0:
```python
import jax
import jax.numpy as jnp
from jax import lax
from jax.sharding import PartitionSpec as P


def taken_in(section, axis, dim, lap, start):

    def gathered(part):
        return lax.all_gather(part, axis, axis=dim, tiled=True)

    return lap(start, jax.tree.map(gathered, section), jnp.int32(0))


def join_panel(carry, left_panel, right_panel):
    return carry + jnp.dot(left_panel, right_panel, preferred_element_type=jnp.float32)


def on_device(tall_factor, wide_factor, target):
    begin = jnp.zeros((tall_factor.shape[0], wide_factor.shape[1]), jnp.float32)
    left_line = lax.all_gather(tall_factor, "gx", axis=1, tiled=True)

    def take_rows(carry, piece, start):
        left_piece = lax.dynamic_slice_in_dim(left_line, start, piece.shape[0], axis=1)
        return join_panel(carry, left_piece, piece)

    total = taken_in(wide_factor, "gy", 0, take_rows, begin)
    product_sum = target - total
    row_power = lax.psum(jnp.sum(product_sum * product_sum, axis=1), "gx")
    product_sum = (
        product_sum
        * lax.rsqrt(row_power / (product_sum.shape[1] * lax.axis_size("gx")) + 1e-06)[:, None]
    )
    return product_sum


def solution(mesh):
    return jax.shard_map(
        on_device,
        mesh=mesh,
        in_specs=(P("gy", "gx"), P("gy", "gx"), P("gy", "gx")),
        out_specs=P("gy", "gx"),
        check_vma=False,
    )
```

profile of v0, /device:TPU:0, one launch (start us, length us, event | category | flops | bytes accessed | tf_op | source)
XLA Modules:
  0.0 155.2 jit_solution(12691582396637993418)
XLA Ops:
  6.5 0.0 all-gather.3.cloned.1.call-start
  6.5 0.7 all-gather.3.cloned.1.call-update
  7.3 0.0 all-gather.5.cloned.1.call-start
  7.3 0.7 all-gather.5.cloned.1.call-update
  8.0 5.3 %copy.4 = f32[1024,1024]{0,1:T(8,128)} copy(f32[1024,1024]{1,0:T(8,128)} %param.5) | data formatting | bytes 8388608 | tf_op args[2]
  13.4 32.8 %all-gather.3.cloned.1.call-done = bf16[1024,2048]{1,0:T(8,128)(2,1)} async-done(((bf16[1024,512]{1,0:T(8,128)(2,1)}), bf16[1024,2048]{1,0:T(8,128)(2,1)}) %all-gather.3.cloned.1.call-update) | async-done | bytes 4194320 | tf_op jit(solution)/shard_map/all_gather | solution.py:21
  46.1 74.9 %all-gather.5.cloned.1.call-done = bf16[2048,1024]{1,0:T(8,128)(2,1)} async-done(((bf16[256,1024]{1,0:T(8,128)(2,1)}), bf16[2048,1024]{1,0:T(8,128)(2,1)}) %all-gather.5.cloned.1.call-update) | async-done | bytes 4194320 | tf_op jit(solution)/shard_map/all_gather | solution.py:10
  121.0 11.3 %multiply_reduce_fusion = (f32[1024]{0:T(1024)S(1)}, f32[1024,1024]{0,1:T(8,128)}) fusion(f32[1024,1024]{0,1:T(8,128)} %copy.4, bf16[1024,2048]{1,0:T(8,128)(2,1)} %all-gather.3.cloned.1.call-done, bf16[2048,1024]{1,0:T(8,128)(2,1)} %all-gather.5.cloned.1.call-done), kind=kOutput, calls=%fused_computation | convolution fusion | flops 4298112000 | bytes 16781312 | tf_op jit(solution)/shard_map/dot_general | solution.py:16
  132.4 5.6 %psum.7 = f32[1024]{0:T(1024)S(1)} all-reduce(f32[1024]{0:T(1024)S(1)} %get-tuple-element.5), channel_id=1, replica_groups=mesh['gy'=8,'gx'=4] {'gx'}, use_global_device_ids=true, to_apply=%region_1.0 | all-reduce | flops 1024 | bytes 8192 | tf_op jit(solution)/shard_map/psum | solution.py:29
  138.0 5.0 %broadcast_multiply_fusion = f32[1024,1024]{0,1:T(8,128)} fusion(f32[1024,1024]{0,1:T(8,128)} %get-tuple-element.6, f32[1024]{0:T(1024)S(1)} %add_rsqrt_fusion), kind=kLoop, calls=%fused_computation.1 | loop fusion | flops 1048576 | bytes 8392704 | tf_op jit(solution)/shard_map/mul | solution.py:31
  143.0 5.3 %copy.5 = f32[1024,1024]{1,0:T(8,128)} copy(f32[1024,1024]{0,1:T(8,128)} %broadcast_multiply_fusion) | data formatting | bytes 8388608 | tf_op jit(solution)/shard_map/mul | solution.py:31
  (1 shorter events, 0.0 us)
Async XLA Ops:
  6.5 39.6 %all-gather.3.cloned.1.call-start = ((), (), s32[]{:S(2)}) async-start(), calls=%async_computation | async-start | bytes 5242880 | tf_op jit(solution)/shard_map/all_gather | solution.py:21
  7.3 113.8 %all-gather.5.cloned.1.call-start = ((), (), s32[]{:S(2)}) async-start(), calls=%async_computation.1 | async-start | bytes 4718592 | tf_op jit(solution)/shard_map/all_gather | solution.py:10
Sparse Core Ops, SparseCore 0:
  8.9 37.1 all-gather.2
  48.2 72.7 all-gather.4
where the time goes:
time: 155 us
  waiting for transfers between devices  109 us (70%)
  between operations  13.4 us (9%)
  matrix products  11.3 us (7%)
  local copies, waits for them, and re-layouts  10.7 us (7%)
  blocking collectives  5.63 us (4%)
  other arithmetic  4.99 us (3%)
    all_gather x1, waiting for transfers between devices, gathered(): return lax.all_gather(part, axis, axis=dim, tiled=True)  74.9 us
    all_gather x1, waiting for transfers between devices, on_device(): left_line = lax.all_gather(tall_factor, 'gx', axis=1, tiled=True)  32.8 us
    dot_general x1, matrix products, join_panel(): jnp.dot(left_panel, right_panel, preferred_element_type=jnp.float32)  11.3 us
    psum x1, blocking collectives, on_device(): row_power = lax.psum(jnp.sum(product_sum * product_sum, axis=1), 'gx')  5.63 us
    unnamed x1, local copies, waits for them, and re-layouts  5.35 us
    mul x1, local copies, waits for them, and re-layouts, on_device(): product_sum * lax.rsqrt(row_power / (product_sum.shape[1] * lax.axis_size...  5.34 us
    mul x1, other arithmetic, on_device(): product_sum * lax.rsqrt(row_power / (product_sum.shape[1] * lax.axis_size...  4.98 us
  transfers between devices with their start and end apart: 2, of which 2 were waited for; matrix products, arithmetic and copies ran while one was open for 3% of the time, Pallas kernels for 0%

commit v1 on v0

--- a/solution.py
+++ b/solution.py
@@ -1,7 +1,23 @@
+import functools
 import jax
 import jax.numpy as jnp
 from jax import lax
 from jax.sharding import PartitionSpec as P
+
+
+def run_the_results(content, mesh_dim):
+    q_n = jax.lax.axis_size(mesh_dim)
+    kept_arr = [None] * q_n
+    kept_arr[q_n - 1] = content
+    pile = tuple(((w, (w + 1) % q_n) for w in range(q_n)))
+    for b in range(q_n - 2, -1, -1):
+        kept_arr[b] = jax.lax.ppermute(kept_arr[b + 1], axis_name=mesh_dim, perm=pile)
+    current_block = jnp.concatenate(kept_arr, 1)
+    x_now = (jax.lax.axis_index(mesh_dim) + 1) * content.shape[1]
+    return jnp.roll(current_block, x_now, 1)
+
+
+_serve_body = functools.partial(run_the_results, mesh_dim="gx")
 
 
 def taken_in(section, axis, dim, lap, start):
@@ -18,7 +34,7 @@
 
 def on_device(tall_factor, wide_factor, target):
     begin = jnp.zeros((tall_factor.shape[0], wide_factor.shape[1]), jnp.float32)
-    left_line = lax.all_gather(tall_factor, "gx", axis=1, tiled=True)
+    left_line = _serve_body(tall_factor)
 
     def take_rows(carry, piece, start):
         left_piece = lax.dynamic_slice_in_dim(left_line, start, piece.shape[0], axis=1)

time: 155 us -> 119 us (0.77)
  waiting for transfers between devices: 109 us -> 61 us
  local copies, waits for them, and re-layouts: 10.7 us -> 22.2 us
    all_gather x1, waiting for transfers between devices: 74.9 us -> 22.5 us  [gathered(): return lax.all_gather(part, axis, axis=dim, tiled=True)]
    ppermute x0 -> x3, waiting for transfers between devices: none -> 37.8 us  [run_the_results(): jax.lax.ppermute(kept_arr[b + 1], axis_name=mesh_dim, perm=pile)]
    all_gather x1 -> x0, waiting for transfers between devices: 32.8 us -> none  [on_device(): left_line = lax.all_gather(tall_factor, 'gx', axis=1, tiled=True)]
    unnamed x1 -> x10, local copies, waits for them, and re-layouts: 5.35 us -> 15.8 us
  transfers between devices with their start and end apart: 2 -> 4, of which waited for: 2 -> 4; matrix products, arithmetic and copies ran while one was open for 3% -> 14% of each run, Pallas kernels for 0% -> 0%
where the time goes in v1:
time: 119 us
  waiting for transfers between devices  61 us (51%)
  local copies, waits for them, and re-layouts  22.2 us (19%)
  between operations  13.4 us (11%)
  matrix products  11.3 us (9%)
  blocking collectives  5.63 us (5%)
  other arithmetic  4.99 us (4%)
    ppermute x3, waiting for transfers between devices, run_the_results(): jax.lax.ppermute(kept_arr[b + 1], axis_name=mesh_dim, perm=pile)  37.8 us
    all_gather x1, waiting for transfers between devices, gathered(): return lax.all_gather(part, axis, axis=dim, tiled=True)  22.5 us
    unnamed x10, local copies, waits for them, and re-layouts  15.8 us
    dot_general x1, matrix products, join_panel(): jnp.dot(left_panel, right_panel, preferred_element_type=jnp.float32)  11.3 us
    psum x1, blocking collectives, on_device(): row_power = lax.psum(jnp.sum(product_sum * product_sum, axis=1), 'gx')  5.63 us
    mul x1, local copies, waits for them, and re-layouts, on_device(): product_sum * lax.rsqrt(row_power / (product_sum.shape[1] * lax.axis_size...  5.34 us
    mul x1, other arithmetic, on_device(): product_sum * lax.rsqrt(row_power / (product_sum.shape[1] * lax.axis_size...  4.98 us
  transfers between devices with their start and end apart: 4, of which 4 were waited for; matrix products, arithmetic and copies ran while one was open for 14% of the time, Pallas kernels for 0%

profile of v1, /device:TPU:0, one launch (start us, length us, event | category | flops | bytes accessed | tf_op | source)
XLA Modules:
  0.0 119.1 jit_solution(4471778392054491980)
XLA Ops:
  6.5 0.0 copy-start
  6.5 0.0 all-gather.2.cloned.1.call-start
  6.5 0.7 all-gather.2.cloned.1.call-update
  7.3 0.5 collective-permute-start
  7.8 14.6 %collective-permute-done = bf16[1024,512]{1,0:T(8,128)(2,1)S(1)} collective-permute-done((bf16[1024,512]{1,0:T(8,128)(2,1)}, bf16[1024,512]{1,0:T(8,128)(2,1)S(1)}, u32[]{:S(2)}, u32[]{:S(2)}) %collective-permute-start) | collective-permute-done | bytes 1048608 | tf_op jit(solution)/shard_map/ppermute | solution.py:14
  22.4 0.0 collective-permute-start.1
  22.5 14.2 %collective-permute-done.1 = bf16[1024,512]{1,0:T(8,128)(2,1)S(1)} collective-permute-done((bf16[1024,512]{1,0:T(8,128)(2,1)S(1)}, bf16[1024,512]{1,0:T(8,128)(2,1)S(1)}, u32[]{:S(2)}, u32[]{:S(2)}) %collective-permute-start.1) | collective-permute-done | bytes 1048608 | tf_op jit(solution)/shard_map/ppermute | solution.py:14
  36.7 0.0 collective-permute-start.2
  36.7 5.3 %copy.4 = f32[1024,1024]{0,1:T(8,128)} copy(f32[1024,1024]{1,0:T(8,128)} %param.5) | data formatting | bytes 8388608 | tf_op args[2]
  42.0 9.0 %collective-permute-done.2 = bf16[1024,512]{1,0:T(8,128)(2,1)} collective-permute-done((bf16[1024,512]{1,0:T(8,128)(2,1)S(1)}, bf16[1024,512]{1,0:T(8,128)(2,1)}, u32[]{:S(2)}, u32[]{:S(2)}) %collective-permute-start.2) | collective-permute-done | bytes 1048608 | tf_op jit(solution)/shard_map/ppermute | solution.py:14
  51.0 2.4 %constant_dynamic-update-slice_fusion.7 = bf16[1024,4096]{1,0:T(8,128)(2,1)} fusion(bf16[1024,512]{1,0:T(8,128)(2,1)} %collective-permute-done.2), kind=kLoop, calls=%fused_computation.12 | loop fusion | bytes 2097152
  53.4 1.1 constant_dynamic-update-slice_fusion.6
  54.5 1.2 constant_dynamic-update-slice_fusion.5
  55.6 0.0 copy-done
  55.6 1.1 constant_dynamic-update-slice_fusion.4
  56.8 2.3 %constant_dynamic-update-slice_fusion.3 = bf16[1024,4096]{1,0:T(8,128)(2,1)} fusion(bf16[1024,4096]{1,0:T(8,128)(2,1)} %constant_dynamic-update-slice_fusion.4, bf16[1024,512]{1,0:T(8,128)(2,1)} %collective-permute-done.2), kind=kLoop, calls=%fused_computation.8 | loop fusion | bytes 2097152
  59.1 1.2 constant_dynamic-update-slice_fusion.2
  60.3 1.1 constant_dynamic-update-slice_fusion.1
  61.4 1.1 constant_dynamic-update-slice_fusion
  62.5 22.5 %all-gather.2.cloned.1.call-done = bf16[2048,1024]{1,0:T(8,128)(2,1)} async-done(((bf16[256,1024]{1,0:T(8,128)(2,1)}), bf16[2048,1024]{1,0:T(8,128)(2,1)}) %all-gather.2.cloned.1.call-update) | async-done | bytes 4194320 | tf_op jit(solution)/shard_map/all_gather | solution.py:26
  85.0 11.3 %multiply_reduce_fusion = (f32[1024]{0:T(1024)S(1)}, f32[1024,1024]{0,1:T(8,128)}) fusion(f32[1024,1024]{0,1:T(8,128)} %copy.4, bf16[2048,1024]{1,0:T(8,128)(2,1)} %all-gather.2.cloned.1.call-done, bf16[1024,4096]{1,0:T(8,128)(2,1)} %constant_dynamic-update-slice_fusion, s32[]{:T(128)S(6)} %select_n.14), kind=kOutput, calls=%fused_computation | convolution fusion | flops 4298112000 | bytes 16781316 | tf_op jit(solution)/shard_map/dot_general | solution.py:32
  96.3 5.6 %psum.7 = f32[1024]{0:T(1024)S(1)} all-reduce(f32[1024]{0:T(1024)S(1)} %get-tuple-element.5), channel_id=1, replica_groups=mesh['gy'=8,'gx'=4] {'gx'}, use_global_device_ids=true, to_apply=%region_1.2 | all-reduce | flops 1024 | bytes 8192 | tf_op jit(solution)/shard_map/psum | solution.py:45
  102.0 5.0 %broadcast_multiply_fusion = f32[1024,1024]{0,1:T(8,128)} fusion(f32[1024,1024]{0,1:T(8,128)} %get-tuple-element.6, f32[1024]{0:T(1024)S(1)} %add_rsqrt_fusion), kind=kLoop, calls=%fused_computation.3 | loop fusion | flops 1048576 | bytes 8392704 | tf_op jit(solution)/shard_map/mul | solution.py:47
  107.0 5.3 %copy.5 = f32[1024,1024]{1,0:T(8,128)} copy(f32[1024,1024]{0,1:T(8,128)} %broadcast_multiply_fusion) | data formatting | bytes 8388608 | tf_op jit(solution)/shard_map/mul | solution.py:47
  (1 shorter events, 0.0 us)
Async XLA Ops:
  6.5 49.1 %copy-start = (bf16[1024,512]{1,0:T(8,128)(2,1)S(1)}, bf16[1024,512]{1,0:T(8,128)(2,1)}, u32[]{:S(2)}) copy-start(bf16[1024,512]{1,0:T(8,128)(2,1)} %param.3) | copy-start | bytes 3145732
  6.5 78.5 %all-gather.2.cloned.1.call-start = ((), (), s32[]{:S(2)}) async-start(), calls=%async_computation | async-start | bytes 4718592 | tf_op jit(solution)/shard_map/all_gather | solution.py:26
  7.3 15.2 %collective-permute-start = (bf16[1024,512]{1,0:T(8,128)(2,1)}, bf16[1024,512]{1,0:T(8,128)(2,1)S(1)}, u32[]{:S(2)}, u32[]{:S(2)}) collective-permute-start(bf16[1024,512]{1,0:T(8,128)(2,1)} %param.3), channel_id=1, source_target_pairs={{0,1},{1,2},{2,3},{3,0},{4,5},{5,6},{6,7},{7,4},{8,9},{9,10},{10,1... | collective-permute-start | bytes 3145736 | tf_op jit(solution)/shard_map/ppermute | solution.py:14
  22.4 14.2 %collective-permute-start.1 = (bf16[1024,512]{1,0:T(8,128)(2,1)S(1)}, bf16[1024,512]{1,0:T(8,128)(2,1)S(1)}, u32[]{:S(2)}, u32[]{:S(2)}) collective-permute-start(bf16[1024,512]{1,0:T(8,128)(2,1)S(1)} %collective-permute-done), channel_id=1, source_target_pairs={{0,1},{1,2},{2,3},{3,0},{4,5},{5,6},{6,7},{7,4},{8,9},{9,10},{10,1... | collective-permute-start | bytes 3145736 | tf_op jit(solution)/shard_map/ppermute | solution.py:14
  36.7 14.3 %collective-permute-start.2 = (bf16[1024,512]{1,0:T(8,128)(2,1)S(1)}, bf16[1024,512]{1,0:T(8,128)(2,1)}, u32[]{:S(2)}, u32[]{:S(2)}) collective-permute-start(bf16[1024,512]{1,0:T(8,128)(2,1)S(1)} %collective-permute-done.1), channel_id=1, source_target_pairs={{0,1},{1,2},{2,3},{3,0},{4,5},{5,6},{6,7},{7,4},{8,9},{9,10},{10,1... | collective-permute-start | bytes 3145736 | tf_op jit(solution)/shard_map/ppermute | solution.py:14
Sparse Core Ops, SparseCore 0:
  9.5 75.4 all-gather.1
